TPU v7x, 32 devices: a whole 2x2x4 slice. The times are simulated.
32 devices in a mesh: gx: 4 (over x, core), gy: 8 (over z, y).
Axes of the slice: x: 2, y: 2, z: 4, core: 2. Of those that a mesh axis runs over, the one named last changes fastest.
Arguments:
- activations: bfloat16 [4096, 8192], P('gx', 'gy'), may hold values from -12 to 12
- out_grads: bfloat16 [4096, 4096], P('gx', 'gy'), may hold values from -12 to 12
- left_roots: float32 [32, 1024, 1024], P(('gx', 'gy')), may hold values from -20 to 20, as said below
- right_roots: float32 [32, 1024, 1024], P(('gx', 'gy')), may hold values from -20 to 20, as said below
Outputs:
- update: bfloat16 [8192, 4096], P(None, 'gy')
Inputs may be any that keep to these rules, and one draw needn't show every extreme that they name: `left_roots`: each block is symmetric positive definite. `right_roots`: each block is symmetric positive definite.
All inputs are finite; a program needn't handle non-finite values.
Results may differ from a plain program's by a relative error of at most 0.001.
Values may be sent and summed in bfloat16 or wider, within the bound.
A program may use at most 128 MiB of HBM per device.

v0:
```python
import jax
import jax.numpy as jnp
from jax import lax
from jax.sharding import PartitionSpec as P

epsilon = 1e-06


def partner(block, axis, distance):
    count = lax.axis_size(axis)
    route = []
    for low in range(count):
        high = low | 1 << distance
        if high != low and high < count:
            route += [(low, high), (high, low)]
    return lax.ppermute(block, axis, route)


def local(activations, out_grads, left_roots, right_roots):
    block_size = left_roots.shape[1]
    half_width = block_size // 2
    parity = lax.axis_index("gy") % 2
    is_even = parity == 0
    gathered = lax.all_gather(activations, "gy", axis=1, tiled=True)
    summed = lax.psum_scatter(
        lax.dot_general(
            gathered, out_grads, (((0,), (0,)), ((), ())), preferred_element_type=jnp.float32
        ),
        "gx",
        scatter_dimension=0,
        tiled=True,
    )
    own_part = lax.dynamic_slice_in_dim(summed, parity * block_size, block_size, 0)
    far_part = lax.dynamic_slice_in_dim(summed, (1 - parity) * block_size, block_size, 0)
    received = partner(far_part, "gy", 0)
    left_block = jnp.where(is_even, own_part, received)
    right_block = jnp.where(is_even, received, own_part)
    grad_block = jnp.concatenate([left_block, right_block], axis=1)
    shaped = jnp.dot(
        jnp.dot(left_roots[0], grad_block, precision=lax.Precision.HIGHEST),
        right_roots[0],
        precision=lax.Precision.HIGHEST,
    )
    graft = jnp.sqrt(jnp.mean(grad_block * grad_block) + epsilon) / jnp.sqrt(
        jnp.mean(shaped * shaped) + epsilon
    )
    finished = (shaped * graft).astype(jnp.bfloat16)
    own_part = lax.dynamic_slice_in_dim(finished, parity * half_width, half_width, 1)
    far_part = lax.dynamic_slice_in_dim(finished, (1 - parity) * half_width, half_width, 1)
    received = partner(far_part, "gy", 0)
    upper_rows = jnp.where(is_even, own_part, received)
    lower_rows = jnp.where(is_even, received, own_part)
    paired = jnp.concatenate([upper_rows, lower_rows], axis=0)
    return lax.all_gather(paired, "gx", axis=0, tiled=True)


def solution(mesh):
    in_specs = (
        P("gx", "gy"),
        P("gx", "gy"),
        P(("gx", "gy"), None, None),
        P(("gx", "gy"), None, None),
    )
    out_specs = P(None, "gy")
    return jax.shard_map(local, mesh=mesh, in_specs=in_specs, out_specs=out_specs, check_vma=False)
```

profile of v0, /device:TPU:0, one launch (start us, length us, event | category | flops | bytes accessed | tf_op | source)
XLA Modules:
  0.0 584.2 jit_solution(13021869417593906638)
XLA Ops:
  6.5 0.0 copy-start
  6.5 0.0 all-gather.3.cloned.1.call-start
  6.5 0.7 all-gather.3.cloned.1.call-update
  7.3 0.0 reduce-scatter.2.cloned.1.call-start
  7.3 232.2 %all-gather.3.cloned.1.call-done = bf16[1024,8192]{1,0:T(8,128)(2,1)} async-done(((bf16[1024,1024]{1,0:T(8,128)(2,1)}), bf16[1024,8192]{1,0:T(8,128)(2,1)}) %all-gather.3.cloned.1.call-update) | async-done | bytes 16777232 | tf_op jit(solution)/shard_map/all_gather | solution.py:24
  239.5 0.0 copy-done
  239.5 15.8 %fusion.5 = f32[8192,512]{1,0:T(8,128)} fusion(bf16[1024,8192]{1,0:T(8,128)(2,1)} %all-gather.3.cloned.1.call-done, bf16[1024,512]{1,0:T(8,128)(2,1)S(1)} %copy-done), kind=kOutput, calls=%fused_computation.16 | convolution fusion | flops 8589934592 | bytes 34603008 | tf_op jit(solution)/shard_map/dot_general | solution.py:26
  255.3 0.0 reduce-scatter.2.cloned.1.call-update
  255.3 0.0 all-gather.5.cloned.1.call-start
  255.4 123.3 %reduce-scatter.2.cloned.1.call-done = f32[2048,512]{1,0:T(8,128)} async-done(((f32[8192,512]{1,0:T(8,128)}), f32[2048,512]{1,0:T(8,128)}) %reduce-scatter.2.cloned.1.call-update) | async-done | bytes 4194320 | tf_op jit(solution)/shard_map/reduce_scatter | solution.py:25
  378.7 3.1 constant_dynamic-slice_fusion.1
  381.8 1.5 collective-permute-start
  383.3 45.9 %collective-permute-done = f32[1024,512]{1,0:T(8,128)S(1)} collective-permute-done((f32[1024,512]{1,0:T(8,128)}, f32[1024,512]{1,0:T(8,128)S(1)}, u32[]{:S(2)}, u32[]{:S(2)}) %collective-permute-start) | collective-permute-done | bytes 2097184 | tf_op jit(solution)/shard_map/ppermute | solution.py:16
  429.2 2.1 dynamic-slice_select_fusion.1
  431.3 0.0 copy-start.2
  431.3 1.7 multiply_reduce_fusion.1
  433.0 0.4 copy-done.2
  433.5 28.3 %fusion.2 = f32[1024,1024]{1,0:T(8,128)} fusion(f32[1,1024,1024]{2,1,0:T(8,128)S(1)} %copy-done.2, f32[1024,512]{1,0:T(8,128)S(1)} %get-tuple-element.6, f32[1024,512]{1,0:T(8,128)S(1)} %get-tuple-element.5), kind=kOutput, calls=%fused_computation.3 | convolution fusion | flops 12885950464 | bytes 12582912 | tf_op jit(solution)/shard_map/dot_general | solution.py:40
  462.5 18.5 %multiply_reduce_fusion = (f32[]{:T(128)}, f32[1024,1024]{1,0:T(8,128)}) fusion(f32[1024,1024]{1,0:T(8,128)} %fusion.2, f32[1,1024,1024]{2,1,0:T(8,128)} %param.7), kind=kOutput, calls=%fused_computation.6 | convolution fusion | flops 12886999040 | bytes 12582916 | tf_op jit(solution)/shard_map/dot_general | solution.py:39
  481.7 2.8 multiply_convert_fusion
  484.5 0.1 constant_dynamic-slice_fusion
  484.6 1.6 collective-permute-start.1
  486.2 22.5 %collective-permute-done.1 = bf16[1024,512]{1,0:T(8,128)(2,1)} collective-permute-done((bf16[1024,512]{1,0:T(8,128)(2,1)S(1)}, bf16[1024,512]{1,0:T(8,128)(2,1)}, u32[]{:S(2)}, u32[]{:S(2)}) %collective-permute-start.1) | collective-permute-done | bytes 1048608 | tf_op jit(solution)/shard_map/ppermute | solution.py:16
  508.6 1.7 broadcast_select_fusion.1
  510.3 1.5 pad_maximum_fusion.2
  511.8 0.0 all-gather.5.cloned.1.call-update
  511.8 58.5 %all-gather.5.cloned.1.call-done = bf16[8192,512]{1,0:T(8,128)(2,1)} async-done(((bf16[2048,512]{1,0:T(8,128)(2,1)}), bf16[8192,512]{1,0:T(8,128)(2,1)}) %all-gather.5.cloned.1.call-update) | async-done | bytes 8388624 | tf_op jit(solution)/shard_map/all_gather | solution.py:54
  570.3 0.0 copy-start.1
  570.3 7.4 %copy.6 = bf16[8192,512]{1,0:T(8,128)(2,1)} copy(bf16[8192,512]{1,0:T(8,128)(2,1)} %all-gather.5.cloned.1.call-done) | data formatting | bytes 16777216
  577.7 0.0 copy-done.1
Async XLA Ops:
  6.5 233.0 %copy-start = (bf16[1024,512]{1,0:T(8,128)(2,1)S(1)}, bf16[1024,512]{1,0:T(8,128)(2,1)}, u32[]{:S(2)}) copy-start(bf16[1024,512]{1,0:T(8,128)(2,1)} %param.5) | copy-start | bytes 3145732
  6.5 233.0 %all-gather.3.cloned.1.call-start = ((), (), s32[]{:S(2)}) async-start(), calls=%async_computation.1 | async-start | bytes 18874368 | tf_op jit(solution)/shard_map/all_gather | solution.py:24
  7.3 371.5 %reduce-scatter.2.cloned.1.call-start = ((), (), s32[]{:S(2)}) async-start(), calls=%async_computation.2 | async-start | bytes 20971520 | tf_op jit(solution)/shard_map/reduce_scatter | solution.py:25
  255.3 315.0 %all-gather.5.cloned.1.call-start = ((), (), s32[]{:S(2)}) async-start(), calls=%async_computation.3 | async-start | bytes 10485760 | tf_op jit(solution)/shard_map/all_gather | solution.py:54
  381.8 47.4 %collective-permute-start = (f32[1024,512]{1,0:T(8,128)}, f32[1024,512]{1,0:T(8,128)S(1)}, u32[]{:S(2)}, u32[]{:S(2)}) collective-permute-start(f32[1024,512]{1,0:T(8,128)} %constant_dynamic-slice_fusion.1), channel_id=1, source_target_pairs={{0,1},{1,0},{2,3},{3,2},{4,5},{5,4},{6,7},{7,6},{8,9},{9,8},{10,11... | collective-permute-start | bytes 6291464 | tf_op jit(solution)/shard_map/ppermute | solution.py:16
  431.3 2.2 copy-start.2
  484.6 24.0 %collective-permute-start.1 = (bf16[1024,512]{1,0:T(8,128)(2,1)S(1)}, bf16[1024,512]{1,0:T(8,128)(2,1)}, u32[]{:S(2)}, u32[]{:S(2)}) collective-permute-start(bf16[1024,512]{1,0:T(8,128)(2,1)S(1)} %constant_dynamic-slice_fusion), channel_id=1, source_target_pairs={{0,1},{1,0},{2,3},{3,2},{4,5},{5,4},{6,7},{7,6},{8,9},{9,8},{10,11... | collective-permute-start | bytes 3145736 | tf_op jit(solution)/shard_map/ppermute | solution.py:16
  570.3 7.4 %copy-start.1 = (bf16[1024,512]{1,0:T(8,128)(2,1)S(1)}, bf16[1024,512]{1,0:T(8,128)(2,1)}, u32[]{:S(2)}) copy-start(bf16[1024,512]{1,0:T(8,128)(2,1)} %param.5) | copy-start | bytes 3145732
Sparse Core Ops, SparseCore 0:
  9.5 229.9 all-gather.2
  255.5 123.2 reduce-scatter.1
  511.9 58.3 all-gather.4
where the time goes:
time: 585 us; the launch traced here: 584 us
  waiting for transfers between devices  483 us (83%)
  matrix products  62.6 us (11%)
  between operations  14.6 us (2%)
  local copies, waits for them, and re-layouts  11 us (2%)
  other arithmetic  9.72 us (2%)
    all_gather x1, waiting for transfers between devices, local(): gathered = lax.all_gather(activations, 'gy', axis=1, tiled=True)  232 us
    reduce_scatter x1, waiting for transfers between devices, local(): lax.psum_scatter(lax.dot_general(gathered, out_grads, (((0,), (0,)), ((),...  123 us
    ppermute x2, waiting for transfers between devices, partner(): return lax.ppermute(block, axis, route)  68.4 us
    all_gather x1, waiting for transfers between devices, local(): return lax.all_gather(paired, 'gx', axis=0, tiled=True)  58.5 us
    dot_general x1, matrix products, local(): jnp.dot(left_roots[0], grad_block, precision=lax.Precision.HIGHEST)  28.3 us
    dot_general x1, matrix products, local(): jnp.dot(jnp.dot(left_roots[0], grad_block, precision=lax.Precision.HIGHES...  18.5 us
    dot_general x1, matrix products, local(): lax.dot_general(gathered, out_grads, (((0,), (0,)), ((), ())), preferred_...  15.8 us
  transfers between devices with their start and end apart: 5, of which 5 were waited for; matrix products, arithmetic and copies ran while one was open for 0% of the time, Pallas kernels for 0%

commit v1 on v0

--- a/solution.py
+++ b/solution.py
@@ -1,9 +1,406 @@
+import functools
+
 import jax
 import jax.numpy as jnp
 from jax import lax
+from jax.experimental import pallas as pl
+from jax.experimental.pallas import tpu as pltpu
 from jax.sharding import PartitionSpec as P
 
 epsilon = 1e-06
+MESH = pl.DeviceIdType.MESH
+f32, bf16 = jnp.float32, jnp.bfloat16
+COLUMN, ROW = (((0,), (0,)), ((), ())), (((1,), (0,)), ((), ()))
+
+
+def dot(a, b, dims=ROW):
+    return lax.dot_general(a, b, dims, preferred_element_type=f32)
+
+
+def split(v):
+    high = v.astype(bf16)
+    return high, (v - high.astype(f32)).astype(bf16)
+
+
+def kernel(
+    planes, parts, a, o, left, right, out,
+    af, tr, oall, stage_l, stage_r, lh, ll, rh, rl, grad, half, shaped, fin, sq_g, sq_s,
+    load_sem, own_sem, src_sem, fwd_sem, tr_sem, cross_sem, af_recv, tr_recv,
+    o_own, o_send, o_recv, out_own, out_send, out_recv,
+):
+    i, j = lax.axis_index("gx"), lax.axis_index("gy")
+    x, c, z, y = i // 2, i % 2, j // 2, j % 2
+    block = left.shape[1]
+    width = block // parts
+    half_width = block // 2
+    last = planes - 1
+
+    def dev(xx, cc, zz, yy):
+        return (2 * xx + cc, 2 * zz + yy)
+
+    def remote(src, dst, send, recv, to):
+        return pltpu.make_async_remote_copy(
+            src_ref=src, dst_ref=dst, send_sem=send, recv_sem=recv, device_id=to, device_id_type=MESH
+        )
+
+    loads = [
+        pltpu.make_async_copy(left.at[0], stage_l, load_sem.at[0]),
+        pltpu.make_async_copy(right.at[0], stage_r, load_sem.at[1]),
+    ]
+
+    def o_slot(xx, cc, yy):
+        columns = pl.ds(pl.multiple_of(yy * half_width, half_width), half_width)
+        return oall.at[2 * xx + cc, :, columns]
+
+    def o_copy(src, slot, number, to):
+        xx, cc, yy = slot
+        return remote(src, o_slot(*slot), o_send.at[number], o_recv.at[4 * xx + 2 * cc + yy], to)
+
+    own, over_x, over_y, over_xy = (x, c, y), (1 - x, c, y), (x, c, 1 - y), (1 - x, c, 1 - y)
+    to_x, to_y, to_core = dev(1 - x, c, z, y), dev(x, c, z, 1 - y), dev(x, 1 - c, z, y)
+    o_local = pltpu.make_async_copy(o, o_slot(*own), o_own)
+    o_own_copies = [o_copy(o, own, 0, to_x), o_copy(o, own, 1, to_y), o_copy(o, own, 2, to_core)]
+    o_relays = [
+        o_copy(o_slot(*over_x), over_x, 3, to_y),
+        o_copy(o_slot(*over_x), over_x, 4, to_core),
+        o_copy(o_slot(*over_y), over_y, 5, to_core),
+        o_copy(o_slot(*over_xy), over_xy, 6, to_core),
+    ]
+
+    def o_wait(slot):
+        o_copy(o_slot(*slot), slot, 0, to_x).wait_recv()
+
+    for copy in o_own_copies:
+        copy.start()
+    o_local.start()
+
+    fx, fc = z // 2, z % 2
+    is_home = jnp.logical_and(x == fx, c == fc)
+    keeps = x == fx
+
+    def source(q):
+        return a.at[:, q * width : (q + 1) * width]
+
+    def home_local(q):
+        return pltpu.make_async_copy(source(q), af.at[i, q], own_sem.at[q])
+
+    def home_remote(q):
+        return remote(source(q), af.at[i, q], src_sem.at[0, q], af_recv.at[i, q], dev(fx, fc, z, y))
+
+    def spread(q, step, kept):
+        number = 1 if step > 0 else 2
+        to = dev(x, fc, z + step, y)
+        if kept:
+            return remote(source(q), af.at[i, q], src_sem.at[number, q], af_recv.at[i, q], to)
+        return remote(source(q), tr.at[c, q], src_sem.at[number, q], tr_recv.at[c, q], to)
+
+    for q in range(parts):
+        for step, inside in ((1, z < last), (-1, z > 0)):
+
+            @pl.when(jnp.logical_and(inside, keeps))
+            def _():
+                spread(q, step, True).start()
+
+            @pl.when(jnp.logical_and(inside, jnp.logical_not(keeps)))
+            def _():
+                spread(q, step, False).start()
+
+        @pl.when(is_home)
+        def _():
+            home_local(q).start()
+
+        @pl.when(jnp.logical_not(is_home))
+        def _():
+            home_remote(q).start()
+
+    for load in loads:
+        load.start()
+
+    zf, zt = i, 2 * (1 - x) + c
+    end = jnp.logical_or(z == 0, z == last)
+    mid = jnp.logical_not(end)
+
+    def away(origin):
+        step = jnp.where(z > origin, 1, -1)
+        goes = jnp.logical_and(z != origin, mid)
+        return step, goes
+
+    step_f, goes_f = away(zf)
+    step_t, goes_t = away(zt)
+
+    def af_forward(cc, q):
+        slot = 2 * x + cc
+        return remote(
+            af.at[slot, q], af.at[slot, q], fwd_sem.at[cc, q], af_recv.at[slot, q],
+            dev(x, c, z + step_f, y),
+        )
+
+    def tr_forward(cc, q):
+        return remote(
+            tr.at[cc, q], tr.at[cc, q], tr_sem.at[cc, q], tr_recv.at[cc, q],
+            dev(x, c, z + step_t, y),
+        )
+
+    def tr_cross(cc, q):
+        slot = 2 * x + cc
+        return remote(
+            tr.at[cc, q], af.at[slot, q], cross_sem.at[cc, q], af_recv.at[slot, q],
+            dev(1 - x, c, z, y),
+        )
+
+    def af_wait(slot, q):
+        remote(
+            af.at[slot, q], af.at[slot, q], fwd_sem.at[0, q], af_recv.at[slot, q], to_x
+        ).wait_recv()
+
+    def pass_tr(q):
+        for cc in range(2):
+            @pl.when(z != zt)
+            def _():
+                remote(
+                    tr.at[cc, q], tr.at[cc, q], tr_sem.at[cc, q], tr_recv.at[cc, q], to_x
+                ).wait_recv()
+                tr_cross(cc, q).start()
+
+            @pl.when(goes_t)
+            def _():
+                tr_forward(cc, q).start()
+
+    def pass_af(q):
+        for cc in range(2):
+            @pl.when(goes_f)
+            def _():
+                af_wait(2 * x + cc, q)
+                af_forward(cc, q).start()
+
+    o_wait(over_x)
+    o_relays[0].start()
+    o_relays[1].start()
+
+    @pl.when(mid)
+    def _():
+        for q in range(parts // 2):
+            pass_tr(q)
+            pass_af(q)
+
+    o_wait(over_y)
+    o_relays[2].start()
+    o_wait(over_xy)
+    o_relays[3].start()
+
+    early = jnp.logical_and(end, jnp.abs(z - zt) > jnp.abs(z - zf))
+
+    @pl.when(mid)
+    def _():
+        for q in range(parts // 2, parts):
+            pass_tr(q)
+            pass_af(q)
+
+    @pl.when(jnp.logical_and(end, jnp.logical_not(early)))
+    def _():
+        for q in range(parts):
+            pass_tr(q)
+
+    for load in loads:
+        load.wait()
+
+    tile = width
+    tiles = block // tile
+
+    @pl.loop(0, tiles)
+    def _(k):
+        rows = pl.ds(pl.multiple_of(k * tile, tile), tile)
+        high, low = split(stage_l[rows, :])
+        lh[rows, :], ll[rows, :] = high, low
+        high, low = split(stage_r[rows, :])
+        rh[rows, :], rl[rows, :] = high, low
+        half[rows, :] = jnp.zeros((tile, block), f32)
+
+    sq_g[...] = jnp.zeros_like(sq_g)
+    sq_s[...] = jnp.zeros_like(sq_s)
+
+    for xx, cc, yy in ((x, 1 - c, y), (1 - x, 1 - c, y), (x, 1 - c, 1 - y), (1 - x, 1 - c, 1 - y)):
+        o_wait((xx, cc, yy))
+    o_local.wait()
+
+    def wait_part(q):
+        for slot in range(4):
+            at_home = z == zf
+
+            @pl.when(jnp.logical_and(at_home, slot == i))
+            def _():
+                home_local(q).wait()
+
+            crossed = jnp.logical_or(slot // 2 != x, end)
+
+            @pl.when(jnp.logical_or(
+                jnp.logical_and(at_home, slot != i),
+                jnp.logical_and(jnp.logical_not(at_home), crossed),
+            ))
+            def _():
+                af_wait(slot, q)
+
+    for q in range(parts):
+        wait_part(q)
+        grad[...] = dot(af[0, q], oall[0], COLUMN)
+
+        @pl.loop(1, 4)
+        def _(k):
+            grad[...] += dot(af[k, q], oall[k], COLUMN)
+
+        sq_g[...] += jnp.sum(grad[...] * grad[...], axis=0, keepdims=True)
+        columns = slice(q * width, (q + 1) * width)
+
+        @pl.loop(0, tiles)
+        def _(k):
+            rows = pl.ds(pl.multiple_of(k * tile, tile), tile)
+            gh, gl = split(grad[...])
+            lhk, llk = lh[rows, columns], ll[rows, columns]
+            half[rows, :] += dot(lhk, gh) + dot(llk, gh) + dot(lhk, gl)
+
+    @pl.when(early)
+    def _():
+        for q in range(parts):
+            pass_tr(q)
+
+    @pl.loop(0, tiles)
+    def _(k):
+        rows = pl.ds(pl.multiple_of(k * tile, tile), tile)
+        th, tl = split(half[rows, :])
+        value = dot(th, rh[...]) + dot(tl, rh[...]) + dot(th, rl[...])
+        shaped[rows, :] = value
+        sq_s[...] += jnp.sum(value * value, axis=0, keepdims=True)
+
+    count = block * block
+    mean_g = jnp.sum(sq_g[...], axis=1, keepdims=True) / count
+    mean_s = jnp.sum(sq_s[...], axis=1, keepdims=True) / count
+    graft = jnp.sqrt(mean_g + epsilon) / jnp.sqrt(mean_s + epsilon)
+
+    def out_slot(slot, p):
+        xx, cc, yy = slot
+        start = (4 * xx + 2 * cc + yy) * block + p * tile
+        return out.at[pl.ds(pl.multiple_of(start, tile), tile), :]
+
+    def out_copy(src, slot, p, number, to):
+        xx, cc, yy = slot
+        return remote(
+            src, out_slot(slot, p), out_send.at[number, p], out_recv.at[4 * xx + 2 * cc + yy, p], to
+        )
+
+    def out_wait(slot, p):
+        out_copy(out_slot(slot, p), slot, p, 0, to_x).wait_recv()
+
+    def fin_part(side, p):
+        columns = pl.ds(pl.multiple_of(side * half_width, half_width), half_width)
+        return fin.at[p * tile : (p + 1) * tile, columns]
+
+    def out_local(p):
+        return pltpu.make_async_copy(fin_part(y, p), out_slot(own, p), out_own.at[p])
+
+    def out_first(p):
+        return [
+            out_copy(fin_part(1 - y, p), own, p, 0, to_y),
+            out_copy(fin_part(y, p), own, p, 1, to_x),
+            out_copy(fin_part(y, p), own, p, 2, to_core),
+        ]
+
+    def out_relay_y(p):
+        return [
+            out_copy(out_slot(over_y, p), over_y, p, 3, to_x),
+            out_copy(out_slot(over_y, p), over_y, p, 4, to_core),
+        ]
+
+    def out_relay_x(p):
+        return out_copy(out_slot(over_x, p), over_x, p, 5, to_core)
+
+    def out_relay_xy(p):
+        return out_copy(out_slot(over_xy, p), over_xy, p, 6, to_core)
+
+    for p in range(tiles):
+        fin[p * tile : (p + 1) * tile, :] = (
+            shaped[p * tile : (p + 1) * tile, :] * graft
+        ).astype(bf16)
+        for copy in out_first(p):
+            copy.start()
+        out_local(p).start()
+    for p in range(tiles):
+        out_wait(over_y, p)
+        for copy in out_relay_y(p):
+            copy.start()
+    for p in range(tiles):
+        out_wait(over_x, p)
+        out_relay_x(p).start()
+    for p in range(tiles):
+        out_wait(over_xy, p)
+        out_relay_xy(p).start()
+    for p in range(tiles):
+        for xx, yy in ((x, y), (x, 1 - y), (1 - x, y), (1 - x, 1 - y)):
+            out_wait((xx, 1 - c, yy), p)
+        out_local(p).wait()
+        for copy in out_first(p) + out_relay_y(p) + [out_relay_x(p), out_relay_xy(p)]:
+            copy.wait_send()
+
+    for copy in o_own_copies + o_relays:
+        copy.wait_send()
+    for q in range(parts):
+        for step, inside in ((1, z < last), (-1, z > 0)):
+            @pl.when(inside)
+            def _():
+                spread(q, step, True).wait_send()
+
+        @pl.when(jnp.logical_not(is_home))
+        def _():
+            home_remote(q).wait_send()
+
+        for cc in range(2):
+            @pl.when(z != zt)
+            def _():
+                tr_cross(cc, q).wait_send()
+
+            @pl.when(goes_t)
+            def _():
+                tr_forward(cc, q).wait_send()
+
+            @pl.when(goes_f)
+            def _():
+                af_forward(cc, q).wait_send()
+
+
+def routed(planes, activations, out_grads, left_roots, right_roots):
+    block = left_roots.shape[1]
+    tokens = activations.shape[0]
+    parts = 4
+    width = block // parts
+    dma = pltpu.SemaphoreType.DMA
+    return pl.pallas_call(
+        functools.partial(kernel, planes, parts),
+        out_shape=jax.ShapeDtypeStruct((planes * 2 * block, block // 2), bf16),
+        in_specs=[pl.BlockSpec(memory_space=pl.ANY)] * 4,
+        out_specs=pl.BlockSpec(memory_space=pl.ANY),
+        scratch_shapes=[
+            pltpu.VMEM((4, parts, tokens, width), bf16),
+            pltpu.VMEM((2, parts, tokens, width), bf16),
+            pltpu.VMEM((4, tokens, block), bf16),
+            pltpu.VMEM((block, block), f32),
+            pltpu.VMEM((block, block), f32),
+            pltpu.VMEM((block, block), bf16),
+            pltpu.VMEM((block, block), bf16),
+            pltpu.VMEM((block, block), bf16),
+            pltpu.VMEM((block, block), bf16),
+            pltpu.VMEM((width, block), f32),
+            pltpu.VMEM((block, block), f32),
+            pltpu.VMEM((block, block), f32),
+            pltpu.VMEM((block, block), bf16),
+            pltpu.VMEM((1, block), f32),
+            pltpu.VMEM((1, block), f32),
+            dma((2,)), dma((parts,)), dma((3, parts)), dma((2, parts)), dma((2, parts)),
+            dma((2, parts)), dma((4, parts)), dma((2, parts)),
+            dma, dma((7,)), dma((8,)), dma((parts,)), dma((7, parts)), dma((8, parts)),
+        ],
+        compiler_params=pltpu.CompilerParams(
+            has_side_effects=True, vmem_limit_bytes=62 * 1024 * 1024
+        ),
+    )(activations, out_grads, left_roots, right_roots)
 
 
 def partner(block, axis, distance):
@@ -62,4 +459,14 @@
         P(("gx", "gy"), None, None),
     )
     out_specs = P(None, "gy")
-    return jax.shard_map(local, mesh=mesh, in_specs=in_specs, out_specs=out_specs, check_vma=False)
+    n_gx, n_gy = mesh.shape["gx"], mesh.shape["gy"]
+
+    def per_device(activations, out_grads, left_roots, right_roots):
+        operands = activations, out_grads, left_roots, right_roots
+        block = left_roots.shape[1]
+        whole_blocks = activations.shape[1] == block and out_grads.shape[1] * 2 == block
+        if n_gx == 4 and n_gy == 2 * n_gx and whole_blocks:
+            return routed(n_gx, *operands)
+        return local(*operands)
+
+    return jax.shard_map(per_device, mesh=mesh, in_specs=in_specs, out_specs=out_specs, check_vma=False)

time: 585 us -> 254 us (0.43)
  waiting for transfers between devices: 483 us -> 0 us
  Pallas kernels: 0 us -> 247 us
  matrix products: 62.6 us -> 0 us
  between operations: 14.6 us -> 0.01 us
  other arithmetic: 9.72 us -> 0 us
    all_gather x2 -> x0, waiting for transfers between devices: 291 us -> none  [the longest x1 232 us: local(): gathered = lax.all_gather(activations, 'gy', axis=1, tiled=True)]
    pallas_call x0 -> x1, Pallas kernels: none -> 247 us  [routed(): pl.pallas_call(functools.partial(kernel, planes, parts), out_shape=jax.Sh...]
    reduce_scatter x1 -> x0, waiting for transfers between devices: 123 us -> none  [local(): lax.psum_scatter(lax.dot_general(gathered, out_grads, (((0,), (0,)), ((),...]
    ppermute x2 -> x0, waiting for transfers between devices: 68.4 us -> none  [partner(): return lax.ppermute(block, axis, route)]
    dot_general x3 -> x0, matrix products: 62.6 us -> none  [the longest x1 28.3 us: local(): jnp.dot(left_roots[0], grad_block, precision=lax.Precision.HIGHEST)]
  transfers between devices with their start and end apart: 5 -> 0, of which waited for: 5 -> 0; matrix products, arithmetic and copies ran while one was open for 0% -> 0% of each run, Pallas kernels for 0% -> 0%
where the time goes in v1:
time: 254 us
  Pallas kernels  247 us (97%)
  local copies, waits for them, and re-layouts  7.32 us (3%)
    pallas_call x1, Pallas kernels, routed(): pl.pallas_call(functools.partial(kernel, planes, parts), out_shape=jax.Sh...  247 us
    unnamed x1, local copies, waits for them, and re-layouts  7.32 us

profile of v1, /device:TPU:0, one launch (start us, length us, event | category | flops | bytes accessed | tf_op | source)
XLA Modules:
  0.0 254.1 jit_solution(9822258466391421705)
XLA Ops:
  0.0 246.8 %shard_map.46 = bf16[8192,512]{1,0:T(8,128)(2,1)} custom-call(bf16[1024,1024]{1,0:T(8,128)(2,1)} %a.1, bf16[1024,512]{1,0:T(8,128)(2,1)} %o.1, f32[1,1024,1024]{2,1,0:T(8,128)} %left.1, f32[1,1024,1024]{2,1,0:T(8,128)} %right.1), custom_call_target="tpu_custom_call" | custom-call | tf_op jit(solution)/shard_map/pallas_call | solution.py:375
  246.8 7.3 %copy.6 = bf16[8192,512]{1,0:T(8,128)(2,1)} copy(bf16[8192,512]{1,0:T(8,128)(2,1)} %shard_map.46) | data formatting | bytes 16777216

commit v2 on v1

--- a/solution.py
+++ b/solution.py
@@ -109,10 +109,6 @@
         def _():
             home_local(q).start()
 
-        @pl.when(jnp.logical_not(is_home))
-        def _():
-            home_remote(q).start()
-
     for load in loads:
         load.start()
 
@@ -176,6 +172,11 @@
     o_wait(over_x)
     o_relays[0].start()
     o_relays[1].start()
+
+    @pl.when(jnp.logical_not(is_home))
+    def _():
+        for q in range(parts):
+            home_remote(q).start()
 
     @pl.when(mid)
     def _():
@@ -241,6 +242,10 @@
                 af_wait(slot, q)
 
     for q in range(parts):
+        @pl.when(early)
+        def _():
+            pass_tr(q)
+
         wait_part(q)
         grad[...] = dot(af[0, q], oall[0], COLUMN)
 
@@ -257,11 +262,6 @@
             gh, gl = split(grad[...])
             lhk, llk = lh[rows, columns], ll[rows, columns]
             half[rows, :] += dot(lhk, gh) + dot(llk, gh) + dot(lhk, gl)
-
-    @pl.when(early)
-    def _():
-        for q in range(parts):
-            pass_tr(q)
 
     @pl.loop(0, tiles)
     def _(k):

time: 254 us -> 220 us (0.87)
  Pallas kernels: 247 us -> 213 us
    pallas_call x1, Pallas kernels: 247 us -> 213 us  [routed(): pl.pallas_call(functools.partial(kernel, planes, parts), out_shape=jax.Sh...]
where the time goes in v2:
time: 220 us
  Pallas kernels  213 us (97%)
  local copies, waits for them, and re-layouts  7.32 us (3%)
    pallas_call x1, Pallas kernels, routed(): pl.pallas_call(functools.partial(kernel, planes, parts), out_shape=jax.Sh...  213 us
    unnamed x1, local copies, waits for them, and re-layouts  7.32 us

profile of v2, /device:TPU:0, one launch (start us, length us, event | category | flops | bytes accessed | tf_op | source)
XLA Modules:
  0.0 220.0 jit_solution(15878465285908569140)
XLA Ops:
  0.0 212.7 %shard_map.46 = bf16[8192,512]{1,0:T(8,128)(2,1)} custom-call(bf16[1024,1024]{1,0:T(8,128)(2,1)} %a.1, bf16[1024,512]{1,0:T(8,128)(2,1)} %o.1, f32[1,1024,1024]{2,1,0:T(8,128)} %left.1, f32[1,1024,1024]{2,1,0:T(8,128)} %right.1), custom_call_target="tpu_custom_call" | custom-call | tf_op jit(solution)/shard_map/pallas_call | solution.py:375
  212.7 7.3 %copy.6 = bf16[8192,512]{1,0:T(8,128)(2,1)} copy(bf16[8192,512]{1,0:T(8,128)(2,1)} %shard_map.46) | data formatting | bytes 16777216

commit v3 on v2

--- a/solution.py
+++ b/solution.py
@@ -205,7 +205,7 @@
     for load in loads:
         load.wait()
 
-    tile = width
+    tile = 2 * width
     tiles = block // tile
 
     @pl.loop(0, tiles)
@@ -369,7 +369,7 @@
 def routed(planes, activations, out_grads, left_roots, right_roots):
     block = left_roots.shape[1]
     tokens = activations.shape[0]
-    parts = 4
+    parts = 8
     width = block // parts
     dma = pltpu.SemaphoreType.DMA
     return pl.pallas_call(

time: 220 us -> 219 us (level)
  no operation moved by 1% of the time
where the time goes in v3:
time: 219 us
  Pallas kernels  211 us (96%)
  local copies, waits for them, and re-layouts  7.32 us (3%)
    pallas_call x1, Pallas kernels, routed(): pl.pallas_call(functools.partial(kernel, planes, parts), out_shape=jax.Sh...  211 us
    unnamed x1, local copies, waits for them, and re-layouts  7.32 us

profile of v3, /device:TPU:0, one launch (start us, length us, event | category | flops | bytes accessed | tf_op | source)
XLA Modules:
  0.0 218.5 jit_solution(5191378304262283355)
XLA Ops:
  0.0 211.2 %shard_map.46 = bf16[8192,512]{1,0:T(8,128)(2,1)} custom-call(bf16[1024,1024]{1,0:T(8,128)(2,1)} %a.1, bf16[1024,512]{1,0:T(8,128)(2,1)} %o.1, f32[1,1024,1024]{2,1,0:T(8,128)} %left.1, f32[1,1024,1024]{2,1,0:T(8,128)} %right.1), custom_call_target="tpu_custom_call" | custom-call | tf_op jit(solution)/shard_map/pallas_call | solution.py:375
  211.2 7.3 %copy.6 = bf16[8192,512]{1,0:T(8,128)(2,1)} copy(bf16[8192,512]{1,0:T(8,128)(2,1)} %shard_map.46) | data formatting | bytes 16777216
